TPU v7x, 32 devices: a whole 2x2x4 slice. The times are simulated.
32 devices in a mesh: chan: 2 (over x), vis: 2 (over core), pix: 8 (over z, y).
Axes of the slice: x: 2, y: 2, z: 4, core: 2. Of those that a mesh axis runs over, the one named last changes fastest.
Arguments:
- response: bfloat16 [16384, 49152], P(('chan', 'vis'), 'pix'), parts along dimension 0, may hold values from -5 to 5
- vis_data: float32 [16384], P(('chan', 'vis')), parts along dimension 0, may hold values from -6 to 6
- baseline_of_row: int32 [8192], P('vis'), may hold values from 0 to 8191
- noise_class: int32 [8192], P('vis'), may hold values from 0 to 15
- baseline_weight: float32 [8192], replicated, may hold values from 0.25 to 4
- class_inv_var: float32 [32], P('chan'), parts along dimension 0, may hold values from 0.25 to 4
Outputs:
- sky_map: float32 [98304], P(('chan', 'pix')), parts along dimension 0
- psf: float32 [98304, 64], P(('chan', 'pix'), 'vis'), parts along dimension 0
There are 2 independent parts, one for each index of `chan`. A program takes and returns all parts, laid end to end along the dimension named above; an argument that names none is the same for every part. Nothing has to cross between parts.
Inputs may be any that keep to these rules, and one draw needn't show every extreme that they name: `baseline_of_row`: baseline index of each row.
All inputs are finite; a program needn't handle non-finite values.
Results may differ from a plain program's by a relative error of at most 0.0041.
Values may be sent and summed in bfloat16 or wider, within the bound.
No kernel may reach another device: no remote copies, remote signals or barrier semaphores. Data moves between devices by JAX's collectives and lax.ppermute only.
A program may use at most 128 MiB of HBM per device.

v0:
```python
import jax
import jax.numpy as jnp
from jax import lax
from jax.sharding import PartitionSpec as P

PANEL_DEV = 8


def shards(response, vis_data, baseline_of_row, noise_class, baseline_weight, class_inv_var):
    classes = lax.broadcasted_iota(jnp.int32, (1, class_inv_var.shape[0]), 1)
    class_weight = jnp.sum(
        jnp.where(noise_class[:, None] == classes, class_inv_var[None, :], jnp.float32(0.0)), axis=1
    )
    weight_row = jnp.take(baseline_weight, baseline_of_row) * class_weight
    own_panel = response[:, :PANEL_DEV]
    pix_rows = response.shape[1]
    piece_cols = lax.all_gather(own_panel, "pix", axis=1, tiled=True)
    operand = (weight_row[:, None] * piece_cols.astype(jnp.float32)).astype(jnp.bfloat16)
    plain_f = piece_cols.astype(jnp.float32)
    beam_part = jnp.concatenate(
        [
            lax.dot_general(
                response, operand, (((0,), (0,)), ((), ())), preferred_element_type=jnp.float32
            ),
            jnp.sum(weight_row[:, None] * plain_f * plain_f, axis=0)[None, :],
        ],
        axis=0,
    )
    weighted_vis = (weight_row * vis_data).astype(jnp.bfloat16)
    dirty_part = jnp.dot(weighted_vis, response, preferred_element_type=jnp.float32)
    norm_part = jnp.sum(weight_row[:, None] * jnp.square(response.astype(jnp.float32)), axis=0)
    col_share = beam_part.shape[1] // lax.axis_size("vis")
    beam_all, dirty_map, pixel_norm = lax.psum((beam_part, dirty_part, norm_part), "vis")
    beam_rows = lax.dynamic_slice_in_dim(beam_all, lax.axis_index("vis") * col_share, col_share, 1)
    panel_scale = beam_rows[pix_rows]
    beam_rows = beam_rows[:pix_rows]
    sky_map = dirty_map / jnp.sqrt(pixel_norm)
    psf = beam_rows / jnp.sqrt(pixel_norm[:, None] * panel_scale[None, :])
    return (sky_map, psf)


def solution(mesh):
    placed = (P(("chan", "vis"), "pix"), P(("chan", "vis")), P("vis"), P("vis"), P(), P("chan"))
    return jax.shard_map(
        shards,
        mesh=mesh,
        in_specs=placed,
        out_specs=(P(("chan", "pix")), P(("chan", "pix"), "vis")),
        check_vma=False,
    )
```

profile of v0, /device:TPU:0, one launch (start us, length us, event | category | flops | bytes accessed | tf_op | source)
XLA Modules:
  0.0 140.9 jit_solution(5494770655249392284)
XLA Ops:
  7.2 0.0 copy-start
  7.2 0.0 all-reduce.3.cloned.1.call-start
  7.2 0.7 fusion.2
  8.0 1.3 slice.9
  9.2 0.3 copy.14
  9.6 33.0 %all_gather.3 = bf16[4096,64]{0,1:T(8,128)(2,1)S(1)} all-gather(bf16[4096,8]{0,1:T(8,128)(2,1)S(1)} %copy.14), channel_id=1, replica_groups=mesh['chan'=2,'vis'=2,'pix'=8] {'pix'}, dimensions={1}, use_global_device_ids=true | all-gather | bytes 589824 | tf_op jit(solution)/shard_map/all_gather | solution.py:17
  42.6 0.0 copy-done
  42.6 23.0 %gather_fusion = f32[4096]{0:T(1024)S(1)} fusion(f32[8192]{0:T(1024)S(1)} %copy-done, s32[4096]{0:T(1024)S(1)} %fusion.2), kind=kCustom, calls=%fused_computation | custom fusion | bytes 49152 | tf_op jit(solution)/shard_map/jit(_take)/gather | solution.py:14
  65.6 0.9 select_reduce_fusion
  66.5 0.8 multiply_convert_fusion.2
  67.2 19.8 %convolution_bitcast_fusion = f32[6144,64]{0,1:T(8,128)S(1)} fusion(bf16[4096,6144]{1,0:T(8,128)(2,1)} %param.6, bf16[4096,64]{0,1:T(8,128)(2,1)S(1)} %all_gather.3, f32[4096]{0:T(1024)S(1)} %get-tuple-element.5), kind=kOutput, calls=%fused_computation.2 | convolution fusion | flops 3222011904 | bytes 52445184 | tf_op jit(solution)/shard_map/dot_general | solution.py:22
  87.1 0.2 fusion
  87.3 0.1 copy.13
  87.4 1.3 pad_maximum_fusion
  88.7 0.0 all-reduce.3.cloned.1.call-update
  88.7 19.3 %multiply_reduce_fusion = f32[6144]{0:T(1024)S(1)} fusion(bf16[4096,6144]{1,0:T(8,128)(2,1)} %param.6, f32[4096]{0:T(1024)S(1)} %get-tuple-element.5), kind=kLoop, calls=%fused_computation.1 | loop fusion | flops 100657152 | bytes 50372608 | tf_op jit(solution)/shard_map/reduce_sum | solution.py:31
  108.0 18.9 %fusion.3 = f32[1,6144]{1,0:T(1,128)S(1)} fusion(bf16[4096,1]{0,1:T(2,128)(2,1)S(1)} %reshape.26, bf16[4096,6144]{1,0:T(8,128)(2,1)} %param.6), kind=kOutput, calls=%fused_computation.17 | convolution fusion | flops 50331648 | bytes 50364416 | tf_op jit(solution)/shard_map/dot_general | solution.py:30
  126.9 3.5 %all-reduce = (f32[6144]{0:T(1024)S(1)}, f32[6144]{0:T(1024)S(1)}) all-reduce(f32[6144]{0:T(1024)S(1)} %bitcast.7, f32[6144]{0:T(1024)S(1)} %multiply_reduce_fusion), channel_id=1, replica_groups=mesh['chan'=2,'vis'=2,'pix'=8] {'vis'}, use_global_device_ids=true, to_apply=%region_1.2 | all-reduce | flops 12288 | bytes 98304 | tf_op jit(solution)/shard_map/psum | solution.py:33
  130.4 0.6 rsqrt_multiply_fusion
  131.1 0.0 all-reduce.3.cloned.1.call-done
  131.1 0.8 dynamic-slice_reduce_fusion
  131.9 2.2 %dynamic-slice_multiply_fusion = f32[6144,32]{0,1:T(8,128)} fusion(f32[6145,64]{0,1:T(8,128)} %all-reduce.3.cloned.1.call-done, s32[]{:T(128)S(6)} %select_n.21, f32[32]{0:T(128)S(1)} %dynamic-slice_reduce_fusion, f32[6144]{0:T(1024)S(1)} %get-tuple-element.3), kind=kLoop, calls=%fused_computation.7 | loop fusion | flops 393216 | bytes 1597572 | tf_op jit(solution)/shard_map/div | solution.py:38
  (1 shorter events, 0.0 us)
Async XLA Ops:
  7.2 35.4 %copy-start = (f32[8192]{0:T(1024)S(1)}, f32[8192]{0:T(1024)}, u32[]{:S(2)}) copy-start(f32[8192]{0:T(1024)} %param.10) | copy-start | bytes 98308
  7.2 123.9 %all-reduce.3.cloned.1.call-start = ((), (), s32[]{:S(2)}) async-start(), calls=%async_computation | async-start | bytes 3211264 | tf_op jit(solution)/shard_map/psum | solution.py:33
Sparse Core Ops, SparseCore 0:
  88.8 21.5 all-reduce.2
where the time goes:
time: 142 us; the launch traced here: 141 us
  matrix products  38.7 us (27%)
  blocking collectives  36.6 us (26%)
  other arithmetic  26 us (18%)
  local copies, waits for them, and re-layouts  25.6 us (18%)
  between operations  14.1 us (10%)
    all_gather x1, blocking collectives, shards(): piece_cols = lax.all_gather(own_panel, 'pix', axis=1, tiled=True)  33 us
    gather x1, local copies, waits for them, and re-layouts, shards(): weight_row = jnp.take(baseline_weight, baseline_of_row) * class_weight  23 us
    dot_general x1, matrix products, shards(): lax.dot_general(response, operand, (((0,), (0,)), ((), ())), preferred_el...  19.8 us
    reduce_sum x1, other arithmetic, shards(): jnp.sum(weight_row[:, None] * jnp.square(response.astype(jnp.float32)), a...  19.3 us
    dot_general x1, matrix products, shards(): jnp.dot(weighted_vis, response, preferred_element_type=jnp.float32)  18.9 us
    psum x1, blocking collectives, shards(): lax.psum((beam_part, dirty_part, norm_part), 'vis')  3.53 us
  transfers between devices with their start and end apart: 1, of which 0 were waited for; matrix products, arithmetic and copies ran while one was open for 28% of the time, Pallas kernels for 0%

commit v1 on v0

--- a/solution.py
+++ b/solution.py
@@ -14,7 +14,12 @@
     weight_row = jnp.take(baseline_weight, baseline_of_row) * class_weight
     own_panel = response[:, :PANEL_DEV]
     pix_rows = response.shape[1]
-    piece_cols = lax.all_gather(own_panel, "pix", axis=1, tiled=True)
+    ring = [own_panel]
+    for hop in range(7):
+        ring.append(lax.ppermute(ring[-1], "pix", [(dev, (dev + 1) % 8) for dev in range(8)]))
+    piece_cols = jnp.roll(
+        jnp.concatenate(ring[::-1], axis=1), (lax.axis_index("pix") + 1) * ring[0].shape[1], axis=1
+    )
     operand = (weight_row[:, None] * piece_cols.astype(jnp.float32)).astype(jnp.bfloat16)
     plain_f = piece_cols.astype(jnp.float32)
     beam_part = jnp.concatenate(

time: 142 us -> 144 us (1.014)
  blocking collectives: 36.6 us -> 3.57 us
  waiting for transfers between devices: 0.02 us -> 31.9 us
  starting transfers between devices: 0.04 us -> 3.14 us
    all_gather x1 -> x0, blocking collectives: 33 us -> none  [shards(): piece_cols = lax.all_gather(own_panel, 'pix', axis=1, tiled=True)]
    ppermute x0 -> x7, waiting for transfers between devices: none -> 31.8 us  [shards(): lax.ppermute(ring[-1], 'pix', [(dev, (dev + 1) % 8) for dev in range(8)])]
    ppermute x0 -> x7, starting transfers between devices: none -> 3.1 us  [shards(): lax.ppermute(ring[-1], 'pix', [(dev, (dev + 1) % 8) for dev in range(8)])]
  transfers between devices with their start and end apart: 1 -> 8, of which waited for: 0 -> 5; matrix products, arithmetic and copies ran while one was open for 28% -> 45% of each run, Pallas kernels for 0% -> 0%
where the time goes in v1:
time: 144 us
  matrix products  39.3 us (27%)
  waiting for transfers between devices  31.9 us (22%)
  other arithmetic  26 us (18%)
  local copies, waits for them, and re-layouts  25.7 us (18%)
  between operations  14.3 us (10%)
  blocking collectives  3.57 us (2%)
  starting transfers between devices  3.14 us (2%)
    ppermute x7, waiting for transfers between devices, shards(): lax.ppermute(ring[-1], 'pix', [(dev, (dev + 1) % 8) for dev in range(8)])  31.8 us
    gather x1, local copies, waits for them, and re-layouts, shards(): weight_row = jnp.take(baseline_weight, baseline_of_row) * class_weight  23 us
    dot_general x1, matrix products, shards(): lax.dot_general(response, operand, (((0,), (0,)), ((), ())), preferred_el...  19.8 us
    dot_general x1, matrix products, shards(): jnp.dot(weighted_vis, response, preferred_element_type=jnp.float32)  19.5 us
    reduce_sum x1, other arithmetic, shards(): jnp.sum(weight_row[:, None] * jnp.square(response.astype(jnp.float32)), a...  19.3 us
    psum x1, blocking collectives, shards(): lax.psum((beam_part, dirty_part, norm_part), 'vis')  3.57 us
    ppermute x7, starting transfers between devices, shards(): lax.ppermute(ring[-1], 'pix', [(dev, (dev + 1) % 8) for dev in range(8)])  3.1 us
  transfers between devices with their start and end apart: 8, of which 5 were waited for; matrix products, arithmetic and copies ran while one was open for 45% of the time, Pallas kernels for 0%

profile of v1, /device:TPU:0, one launch (start us, length us, event | category | flops | bytes accessed | tf_op | source)
XLA Modules:
  0.0 143.8 jit_solution(15782780012321286393)
XLA Ops:
  7.2 0.0 copy-start
  7.2 0.0 all-reduce.3.cloned.1.call-start
  7.2 1.3 slice.9
  8.5 0.3 copy.14
  8.8 3.0 %collective-permute-start = (bf16[4096,8]{0,1:T(8,128)(2,1)S(1)}, bf16[4096,8]{0,1:T(8,128)(2,1)S(1)}, u32[]{:S(2)}, u32[]{:S(2)}) collective-permute-start(bf16[4096,8]{0,1:T(8,128)(2,1)S(1)} %copy.14), channel_id=1, source_target_pairs={{0,1},{1,2},{2,3},{3,4},{4,5},{5,6},{6,7},{7,0},{8,9},{9,10},{10,1... | collective-permute-start | bytes 196616 | tf_op jit(solution)/shard_map/ppermute | solution.py:19
  11.9 5.3 %collective-permute-done = bf16[4096,8]{0,1:T(8,128)(2,1)S(1)} collective-permute-done((bf16[4096,8]{0,1:T(8,128)(2,1)S(1)}, bf16[4096,8]{0,1:T(8,128)(2,1)S(1)}, u32[]{:S(2)}, u32[]{:S(2)}) %collective-permute-start) | collective-permute-done | bytes 65568 | tf_op jit(solution)/shard_map/ppermute | solution.py:19
  17.1 0.0 collective-permute-start.1
  17.1 7.0 %collective-permute-done.1 = bf16[4096,8]{0,1:T(8,128)(2,1)S(1)} collective-permute-done((bf16[4096,8]{0,1:T(8,128)(2,1)S(1)}, bf16[4096,8]{0,1:T(8,128)(2,1)S(1)}, u32[]{:S(2)}, u32[]{:S(2)}) %collective-permute-start.1) | collective-permute-done | bytes 65568 | tf_op jit(solution)/shard_map/ppermute | solution.py:19
  24.1 0.0 collective-permute-start.2
  24.1 7.0 %collective-permute-done.2 = bf16[4096,8]{0,1:T(8,128)(2,1)S(1)} collective-permute-done((bf16[4096,8]{0,1:T(8,128)(2,1)S(1)}, bf16[4096,8]{0,1:T(8,128)(2,1)S(1)}, u32[]{:S(2)}, u32[]{:S(2)}) %collective-permute-start.2) | collective-permute-done | bytes 65568 | tf_op jit(solution)/shard_map/ppermute | solution.py:19
  31.1 0.0 collective-permute-start.3
  31.1 0.7 fusion.3
  31.8 23.0 %gather_fusion = f32[4096]{0:T(1024)S(1)} fusion(f32[8192]{0:T(1024)S(1)} %copy-done, s32[4096]{0:T(1024)S(1)} %fusion.3), kind=kCustom, calls=%fused_computation | custom fusion | bytes 49152 | tf_op jit(solution)/shard_map/jit(_take)/gather | solution.py:14
  54.8 0.0 collective-permute-done.3
  54.8 0.1 collective-permute-start.4
  54.9 0.9 select_reduce_fusion
  55.8 6.1 %collective-permute-done.4 = bf16[4096,8]{0,1:T(8,128)(2,1)S(1)} collective-permute-done((bf16[4096,8]{0,1:T(8,128)(2,1)S(1)}, bf16[4096,8]{0,1:T(8,128)(2,1)S(1)}, u32[]{:S(2)}, u32[]{:S(2)}) %collective-permute-start.4) | collective-permute-done | bytes 65568 | tf_op jit(solution)/shard_map/ppermute | solution.py:19
  61.9 0.0 collective-permute-start.5
  61.9 0.7 multiply_convert_fusion.2
  62.6 6.6 %collective-permute-done.5 = bf16[4096,8]{0,1:T(8,128)(2,1)S(1)} collective-permute-done((bf16[4096,8]{0,1:T(8,128)(2,1)S(1)}, bf16[4096,8]{0,1:T(8,128)(2,1)S(1)}, u32[]{:S(2)}, u32[]{:S(2)}) %collective-permute-start.5) | collective-permute-done | bytes 65568 | tf_op jit(solution)/shard_map/ppermute | solution.py:19
  69.2 0.0 collective-permute-start.6
  69.2 19.3 %multiply_reduce_fusion = f32[6144]{0:T(1024)S(1)} fusion(bf16[4096,6144]{1,0:T(8,128)(2,1)} %param.6, f32[4096]{0:T(1024)S(1)} %get-tuple-element.5), kind=kLoop, calls=%fused_computation.1 | loop fusion | flops 100657152 | bytes 50372608 | tf_op jit(solution)/shard_map/reduce_sum | solution.py:36
  88.7 19.8 %convolution_bitcast_fusion = f32[6144,64]{0,1:T(8,128)S(1)} fusion(bf16[4096,6144]{1,0:T(8,128)(2,1)} %param.6, f32[4096]{0:T(1024)S(1)} %get-tuple-element.5, bf16[4096,128]{0,1:T(8,128)(2,1)S(1)} %constant_dynamic-update-slice_fusion, s32[]{:T(128)S(6)} %select_n.35), kind=kOutput, calls=%fused_computation.2 | convolution fusion | flops 3222011904 | bytes 52445188 | tf_op jit(solution)/shard_map/dot_general | solution.py:27
  108.6 0.3 fusion
  108.8 0.1 copy.13
  108.9 1.3 pad_maximum_fusion
  110.2 0.0 all-reduce.3.cloned.1.call-update
  110.2 19.5 %fusion.5 = f32[1,6144]{1,0:T(1,128)S(1)} fusion(bf16[4096,1]{0,1:T(2,128)(2,1)S(1)} %reshape.26, bf16[4096,6144]{1,0:T(8,128)(2,1)} %param.6), kind=kOutput, calls=%fused_computation.35 | convolution fusion | flops 50331648 | bytes 50364416 | tf_op jit(solution)/shard_map/dot_general | solution.py:35
  129.7 3.6 %all-reduce = (f32[6144]{0:T(1024)S(1)}, f32[6144]{0:T(1024)S(1)}) all-reduce(f32[6144]{0:T(1024)S(1)} %bitcast.7, f32[6144]{0:T(1024)S(1)} %multiply_reduce_fusion), channel_id=1, replica_groups=mesh['chan'=2,'vis'=2,'pix'=8] {'vis'}, use_global_device_ids=true, to_apply=%region_1.2 | all-reduce | flops 12288 | bytes 98304 | tf_op jit(solution)/shard_map/psum | solution.py:38
  133.3 0.6 rsqrt_multiply_fusion
  133.9 0.8 dynamic-slice_reduce_fusion
  134.8 2.2 %dynamic-slice_multiply_fusion = f32[6144,32]{0,1:T(8,128)} fusion(f32[6145,64]{0,1:T(8,128)} %all-reduce.3.cloned.1.call-done, s32[]{:T(128)S(6)} %select_n.36, f32[32]{0:T(128)S(1)} %dynamic-slice_reduce_fusion, f32[6144]{0:T(1024)S(1)} %get-tuple-element.3), kind=kLoop, calls=%fused_computation.7 | loop fusion | flops 393216 | bytes 1597572 | tf_op jit(solution)/shard_map/div | solution.py:43
  (20 shorter events, 0.1 us)
Async XLA Ops:
  7.2 24.6 %copy-start = (f32[8192]{0:T(1024)S(1)}, f32[8192]{0:T(1024)}, u32[]{:S(2)}) copy-start(f32[8192]{0:T(1024)} %param.10) | copy-start | bytes 98308
  7.2 126.7 %all-reduce.3.cloned.1.call-start = ((), (), s32[]{:S(2)}) async-start(), calls=%async_computation | async-start | bytes 3211264 | tf_op jit(solution)/shard_map/psum | solution.py:38
  8.8 8.3 %collective-permute-start = (bf16[4096,8]{0,1:T(8,128)(2,1)S(1)}, bf16[4096,8]{0,1:T(8,128)(2,1)S(1)}, u32[]{:S(2)}, u32[]{:S(2)}) collective-permute-start(bf16[4096,8]{0,1:T(8,128)(2,1)S(1)} %copy.14), channel_id=1, source_target_pairs={{0,1},{1,2},{2,3},{3,4},{4,5},{5,6},{6,7},{7,0},{8,9},{9,10},{10,1... | collective-permute-start | bytes 196616 | tf_op jit(solution)/shard_map/ppermute | solution.py:19
  17.1 7.0 %collective-permute-start.1 = (bf16[4096,8]{0,1:T(8,128)(2,1)S(1)}, bf16[4096,8]{0,1:T(8,128)(2,1)S(1)}, u32[]{:S(2)}, u32[]{:S(2)}) collective-permute-start(bf16[4096,8]{0,1:T(8,128)(2,1)S(1)} %collective-permute-done), channel_id=1, source_target_pairs={{0,1},{1,2},{2,3},{3,4},{4,5},{5,6},{6,7},{7,0},{8,9},{9,10},{10,1... | collective-permute-start | bytes 196616 | tf_op jit(solution)/shard_map/ppermute | solution.py:19
  24.1 7.0 %collective-permute-start.2 = (bf16[4096,8]{0,1:T(8,128)(2,1)S(1)}, bf16[4096,8]{0,1:T(8,128)(2,1)S(1)}, u32[]{:S(2)}, u32[]{:S(2)}) collective-permute-start(bf16[4096,8]{0,1:T(8,128)(2,1)S(1)} %collective-permute-done.1), channel_id=1, source_target_pairs={{0,1},{1,2},{2,3},{3,4},{4,5},{5,6},{6,7},{7,0},{8,9},{9,10},{10,1... | collective-permute-start | bytes 196616 | tf_op jit(solution)/shard_map/ppermute | solution.py:19
  31.1 23.8 %collective-permute-start.3 = (bf16[4096,8]{0,1:T(8,128)(2,1)S(1)}, bf16[4096,8]{0,1:T(8,128)(2,1)S(1)}, u32[]{:S(2)}, u32[]{:S(2)}) collective-permute-start(bf16[4096,8]{0,1:T(8,128)(2,1)S(1)} %collective-permute-done.2), channel_id=1, source_target_pairs={{0,1},{1,2},{2,3},{3,4},{4,5},{5,6},{6,7},{7,0},{8,9},{9,10},{10,1... | collective-permute-start | bytes 196616 | tf_op jit(solution)/shard_map/ppermute | solution.py:19
  54.8 7.0 %collective-permute-start.4 = (bf16[4096,8]{0,1:T(8,128)(2,1)S(1)}, bf16[4096,8]{0,1:T(8,128)(2,1)S(1)}, u32[]{:S(2)}, u32[]{:S(2)}) collective-permute-start(bf16[4096,8]{0,1:T(8,128)(2,1)S(1)} %collective-permute-done.3), channel_id=1, source_target_pairs={{0,1},{1,2},{2,3},{3,4},{4,5},{5,6},{6,7},{7,0},{8,9},{9,10},{10,1... | collective-permute-start | bytes 196616 | tf_op jit(solution)/shard_map/ppermute | solution.py:19
  61.9 7.3 %collective-permute-start.5 = (bf16[4096,8]{0,1:T(8,128)(2,1)S(1)}, bf16[4096,8]{0,1:T(8,128)(2,1)S(1)}, u32[]{:S(2)}, u32[]{:S(2)}) collective-permute-start(bf16[4096,8]{0,1:T(8,128)(2,1)S(1)} %collective-permute-done.4), channel_id=1, source_target_pairs={{0,1},{1,2},{2,3},{3,4},{4,5},{5,6},{6,7},{7,0},{8,9},{9,10},{10,1... | collective-permute-start | bytes 196616 | tf_op jit(solution)/shard_map/ppermute | solution.py:19
  69.2 19.3 %collective-permute-start.6 = (bf16[4096,8]{0,1:T(8,128)(2,1)S(1)}, bf16[4096,8]{0,1:T(8,128)(2,1)S(1)}, u32[]{:S(2)}, u32[]{:S(2)}) collective-permute-start(bf16[4096,8]{0,1:T(8,128)(2,1)S(1)} %collective-permute-done.5), channel_id=1, source_target_pairs={{0,1},{1,2},{2,3},{3,4},{4,5},{5,6},{6,7},{7,0},{8,9},{9,10},{10,1... | collective-permute-start | bytes 196616 | tf_op jit(solution)/shard_map/ppermute | solution.py:19
Sparse Core Ops, SparseCore 0:
  110.3 22.1 all-reduce.2
